TPU v7x, 32 devices: a whole 2x2x4 slice. The times are simulated.
32 devices in a mesh: gx: 4 (over z), gy: 4 (over y, x), gz: 2 (over core).
Axes of the slice: x: 2, y: 2, z: 4, core: 2. Of those that a mesh axis runs over, the one named last changes fastest.
Arguments:
- panel: float32 [8192, 4096], P(('gx', 'gy', 'gz'))
- treat_start: int32 [8192], P(('gx', 'gy', 'gz')), may hold values from 1024 to 4096
- loading_init: float32 [64, 8192], P(None, ('gx', 'gy', 'gz'))
- factor_init: float32 [64, 4096], P(None, ('gx', 'gy', 'gz'))
- unit_init: float32 [8192], P(('gx', 'gy', 'gz'))
- day_init: float32 [4096], replicated
Outputs:
- loading_out: float32 [64, 8192], P(None, ('gx', 'gy', 'gz'))
- factor_out: float32 [64, 4096], P(None, ('gx', 'gy', 'gz'))
- unit_out: float32 [8192], P(('gx', 'gy', 'gz'))
- day_out: float32 [4096], replicated
Inputs may be any that keep to these rules, and one draw needn't show every extreme that they name: A unit is treated from day treat_start on; 4096 means never treated.
All inputs are finite; a program needn't handle non-finite values.
Results may differ from a plain program's by a relative error of at most 0.0001.
Values sent between devices are 32-bit elements; how exact they have to be, the bound alone decides.
A program may use at most 64 MiB of HBM per device.

v0:
```python
import functools

import jax
import jax.numpy as jnp
from jax import lax
from jax.experimental import pallas as pl
from jax.experimental.pallas import tpu as pltpu
from jax.sharding import PartitionSpec as P

SWEEPS = 2
RIDGE = 1.0
GATHER_PIECES = 2
REDUCE_PIECES = 3
AXES = ("gx", "gy", "gz")
MESH = pl.DeviceIdType.MESH
VMEM = pl.BlockSpec(memory_space=pltpu.VMEM)


def peers(shape):
    here = {axis: lax.axis_index(axis) for axis in AXES}
    found = {}
    for axis in AXES:
        found[axis] = []
        for step in range(1, shape[axis]):
            there = dict(here)
            there[axis] = lax.rem(here[axis] + step, shape[axis])
            found[axis].append((step, there[axis], tuple(there[name] for name in AXES)))
    return here, found


def meet(found):
    barrier = pltpu.get_barrier_semaphore()
    count = 0
    for axis in AXES:
        for _, _, device in found[axis]:
            pl.semaphore_signal(barrier, inc=1, device_id=device, device_id_type=MESH)
            count += 1
    pl.semaphore_wait(barrier, count)


def send_all(found, source, target, send, recv, base):
    copies = []
    for slot, (step, there, device) in enumerate(found):
        copies.append(pltpu.make_async_remote_copy(
            source(step, there), target(step), send.at[base + slot], recv.at[base + slot],
            device_id=device, device_id_type=MESH))
    for copy in copies:
        copy.start()
    return copies


def finish(copies):
    for copy in copies:
        copy.wait()


def spread(block, place, found, send, recv, base):
    mine = block.at[place]
    return send_all(found, lambda step, there: mine, lambda step: mine, send, recv, base)


def gather_kernel(shape, own_ref, out_ref, blocks, send, recv, local):
    here, found = peers(shape)
    z, y, x = here["gz"], here["gy"], here["gx"]
    pieces, rows = blocks.shape[0], blocks.shape[4]
    width = own_ref.shape[1]
    starts = []
    for p in range(pieces):
        starts.append(pltpu.make_async_copy(own_ref.at[p * rows:(p + 1) * rows], blocks.at[p, z, y, x], local.at[p]))
        starts[p].start()
    meet(found)
    moving = [[copy] for copy in starts]
    index = 0
    for axis, place in (("gx", (z, y, x)), ("gy", (z, y)), ("gz", (z,))):
        for p in range(pieces):
            finish(moving[p])
            moving[p] = spread(blocks.at[p], place, found[axis], send, recv, index)
            index += len(found[axis])
    for p in range(pieces):
        finish(moving[p])
        flat = 0
        for x in range(shape["gx"]):
            for y in range(shape["gy"]):
                for z in range(shape["gz"]):
                    out_ref[p * rows:(p + 1) * rows, flat * width:(flat + 1) * width] = blocks[p, z, y, x]
                    flat += 1


def reduce_kernel(shape, part_ref, out_ref, hold_z, hold_y, hold_x, sum_z, sum_y, send, recv):
    here, found = peers(shape)
    z, y, x = here["gz"], here["gy"], here["gx"]
    pieces = part_ref.shape[0]
    meet(found)
    index = 0
    moving = [[] for _ in range(pieces)]
    for axis, source, hold in (("gz", part_ref, hold_z), ("gy", sum_z, hold_y), ("gx", sum_y, hold_x)):
        for p in range(pieces):
            if axis == "gy":
                finish(moving[p])
                value = part_ref[p, z]
                for slot in range(shape["gz"] - 1):
                    value = value + hold_z[p, slot]
                sum_z[p] = value
            if axis == "gx":
                finish(moving[p])
                value = sum_z[p, y]
                for slot in range(shape["gy"] - 1):
                    value = value + hold_y[p, slot]
                sum_y[p] = value
            moving[p] = send_all(
                found[axis], lambda step, there: source.at[p, there], lambda step: hold.at[p, step - 1],
                send, recv, index)
            index += len(found[axis])
    for axis, place in (("gx", (z, y, x)), ("gy", (z, y)), ("gz", (z,))):
        for p in range(pieces):
            finish(moving[p])
            if axis == "gx":
                value = sum_y[p, x]
                for slot in range(shape["gx"] - 1):
                    value = value + hold_x[p, slot]
                out_ref[p, z, y, x] = value
            moving[p] = spread(out_ref.at[p], place, found[axis], send, recv, index)
            index += len(found[axis])
    for p in range(pieces):
        finish(moving[p])


def links(shape):
    return sum(shape[axis] - 1 for axis in AXES)


def gather(shape, own):
    pieces = GATHER_PIECES
    rows, width = own.shape
    devices = shape["gx"] * shape["gy"] * shape["gz"]
    count = pieces * links(shape)
    return pl.pallas_call(
        functools.partial(gather_kernel, shape),
        out_shape=jax.ShapeDtypeStruct((rows, devices * width), own.dtype),
        in_specs=[VMEM],
        out_specs=VMEM,
        scratch_shapes=[
            pltpu.VMEM((pieces, shape["gz"], shape["gy"], shape["gx"], rows // pieces, width), own.dtype),
            pltpu.SemaphoreType.DMA((count,)), pltpu.SemaphoreType.DMA((count,)), pltpu.SemaphoreType.DMA((pieces,)),
        ],
        compiler_params=pltpu.CompilerParams(collective_id=0, has_side_effects=True),
        name="gather_days",
    )(own)


def reduce_all(shape, part):
    z, y, x = shape["gz"], shape["gy"], shape["gx"]
    pieces = REDUCE_PIECES
    tiles = part.shape[0]
    block = (tiles // (pieces * z * y * x),) + part.shape[1:]
    count = 2 * pieces * links(shape)
    f32 = jnp.float32
    total = pl.pallas_call(
        functools.partial(reduce_kernel, shape),
        out_shape=jax.ShapeDtypeStruct((pieces, z, y, x) + block, f32),
        in_specs=[VMEM],
        out_specs=VMEM,
        scratch_shapes=[
            pltpu.VMEM((pieces, z - 1, y, x) + block, f32),
            pltpu.VMEM((pieces, y - 1, x) + block, f32),
            pltpu.VMEM((pieces, x - 1) + block, f32),
            pltpu.VMEM((pieces, y, x) + block, f32),
            pltpu.VMEM((pieces, x) + block, f32),
            pltpu.SemaphoreType.DMA((count,)),
            pltpu.SemaphoreType.DMA((count,)),
        ],
        compiler_params=pltpu.CompilerParams(collective_id=1, has_side_effects=True),
        name="reduce_all",
    )(part.reshape((pieces, z, y, x) + block))
    return total.reshape(part.shape)


def halves(value):
    high = value.astype(jnp.bfloat16)
    return high, (value - high.astype(jnp.float32)).astype(jnp.bfloat16)


def mul(left, right, at):
    return lax.dot_general(left, right, ((at[:1], at[1:]), ((), ())), preferred_element_type=jnp.float32)


def wide_left(value):
    high, low = halves(value)
    return jnp.concatenate([high, high, low], 1)


def wide_right(value):
    high, low = halves(value)
    return jnp.concatenate([high, low, high], 0)


def tall_dot(left, right, at):
    rows = left.shape[0]
    left_high, left_low = halves(left)
    right_high, right_low = halves(right)
    both = mul(jnp.concatenate([left_high, left_low], 0), right_high, (1, at))
    return both[:rows] + both[rows:] + mul(left_high, right_low, (1, at))


def invert(work):
    rank = work.shape[0]
    row_at = lax.broadcasted_iota(jnp.int32, work.shape, 0)
    for k in range(rank):
        pivot_row = work[k:k + 1, :] * (1.0 / work[k:k + 1, k:k + 1])
        work = jnp.where(row_at == k, pivot_row, work - work[:, k:k + 1] * pivot_row)
    return work[:, rank:]


def with_identity(matrix):
    rank = matrix.shape[0]
    eye = jnp.where(
        lax.broadcasted_iota(jnp.int32, (rank, rank), 0) == lax.broadcasted_iota(jnp.int32, (rank, rank), 1), 1.0, 0.0)
    return jnp.concatenate([matrix + RIDGE * eye, eye], 1)


def impute_kernel(width, panel_ref, treat_ref, load_ref, fac_ref, unit_ref, day_ref, part_ref, cent_ref, mean_ref):
    units, days = panel_ref.shape
    rank = load_ref.shape[0]
    lanes = part_ref.shape[2]
    across = days // lanes
    each = width // lanes
    extra = rank // 8 * across
    per = -(-rank // across)
    load = load_ref[...]
    turned = load.T
    load_wide = wide_left(turned)
    part_ref[extra:] = jnp.zeros((part_ref.shape[0] - extra,) + part_ref.shape[1:], jnp.float32)

    def first(tile, total):
        start = pl.multiple_of(tile * width, width)
        cols = pl.ds(start, width)
        fitted = mul(load_wide, wide_right(fac_ref[:, cols]), (1, 0))
        day = lax.broadcasted_iota(jnp.int32, (units, width), 1) + start
        imputed = jnp.where(day < treat_ref[...], panel_ref[:, cols], unit_ref[...] + day_ref[:, cols] + fitted)
        cent_ref[:, cols] = imputed
        without = imputed - fitted
        sums = jnp.sum(without, 0, keepdims=True)
        for c in range(each):
            span = slice(c * lanes, (c + 1) * lanes)
            part_ref[extra + tile * each + c, 0:1, :] = sums[:, span]
            total = total + without[:, span]
        return total

    total = lax.fori_loop(0, days // width, first, jnp.zeros((units, lanes), jnp.float32))
    mean = jnp.sum(total, 1, keepdims=True) / days
    mean_ref[...] = mean

    def second(tile, _):
        cols = pl.ds(pl.multiple_of(tile * width, width), width)
        centred = cent_ref[:, cols] - mean
        cent_ref[:, cols] = centred
        weighted = tall_dot(load, centred, 0)
        for r in range(rank // 8):
            for c in range(each):
                part_ref[r * across + tile * each + c] = weighted[r * 8:r * 8 + 8, c * lanes:(c + 1) * lanes]
        return 0

    lax.fori_loop(0, days // width, second, 0)
    gram = tall_dot(load, load, 1)
    part_ref[extra, 1:2, 0:rank] = jnp.sum(turned, 0, keepdims=True)
    for c in range(-(-rank // per)):
        part_ref[extra + c, 2:2 + per, 0:rank] = gram[c * per:(c + 1) * per]


def solve_kernel(width, devices, total_ref, cent_ref, mean_ref, load_ref, fac_ref, unit_ref, day_ref, gram, shift):
    units, days = cent_ref.shape
    rank = load_ref.shape[0]
    lanes = total_ref.shape[2]
    across = days // lanes
    each = width // lanes
    extra = rank // 8 * across
    per = -(-rank // across)
    for c in range(across):
        shift[0:1, c * lanes:(c + 1) * lanes] = total_ref[extra + c, 0:1, :]
    for c in range(-(-rank // per)):
        gram[c * per:(c + 1) * per, :] = total_ref[extra + c, 2:2 + per, :]
    sums = shift[...]
    grand = jnp.sum(sums, 1, keepdims=True) / (units * devices * days)
    day_eff = sums / (units * devices) - grand
    day_ref[...] = day_eff
    shift[...] = grand - day_eff
    unit_ref[...] = mean_ref[...] - grand
    inverse = wide_left(invert(with_identity(gram[:, 0:rank])))
    same = lax.broadcasted_iota(jnp.int32, (rank, rank), 0) == lax.broadcasted_iota(jnp.int32, (rank, rank), 1)
    load_sum = jnp.sum(jnp.where(same, total_ref[extra, 1:2, 0:rank], 0.0), 1, keepdims=True)

    def step(tile, carry):
        square, projected = carry
        cols = pl.ds(pl.multiple_of(tile * width, width), width)
        weighted = jnp.concatenate([
            jnp.concatenate([total_ref[r * across + tile * each + c] for c in range(each)], 1)
            for r in range(rank // 8)], 0)
        moved = shift[:, cols]
        factors = mul(inverse, wide_right(weighted + load_sum * moved), (1, 0))
        fac_ref[:, cols] = factors
        square = square + tall_dot(factors, factors, 1)
        projected = projected + tall_dot(factors, cent_ref[:, cols] + moved, 1)
        return square, projected

    square, projected = lax.fori_loop(
        0, days // width, step, (jnp.zeros((rank, rank), jnp.float32), jnp.zeros((rank, units), jnp.float32)))
    load_ref[...] = mul(wide_left(invert(with_identity(square))), wide_right(projected), (1, 0))


def body(shape, panel, treat_start, loading_init, factor_init, unit_init, day_init):
    units, days = panel.shape
    devices = shape["gx"] * shape["gy"] * shape["gz"]
    rank, slice_days = factor_init.shape
    lanes = 128
    tiles = (rank // 8 + 1) * (days // lanes)
    tiles = -(-tiles // (REDUCE_PIECES * devices)) * REDUCE_PIECES * devices
    width = min(512, days)
    f32 = jnp.float32

    def array(*sizes):
        return jax.ShapeDtypeStruct(sizes, f32)

    impute = pl.pallas_call(
        functools.partial(impute_kernel, width),
        out_shape=(array(tiles, 8, lanes), array(units, days), array(units, 1)),
        in_specs=[VMEM] * 6,
        out_specs=(VMEM,) * 3,
        name="impute",
    )
    solve = pl.pallas_call(
        functools.partial(solve_kernel, width, devices),
        out_shape=(array(rank, units), array(rank, days), array(units, 1), array(1, days)),
        in_specs=[VMEM] * 3,
        out_specs=(VMEM,) * 4,
        scratch_shapes=[pltpu.VMEM((rank, lanes), f32), pltpu.VMEM((1, days), f32)],
        name="solve",
    )
    treat = treat_start[:, None]
    loading, unit_eff, day_eff = loading_init, unit_init[:, None], day_init[None, :]
    factors = gather(shape, factor_init)
    for _ in range(SWEEPS):
        part, centred, mean = impute(panel, treat, loading, factors, unit_eff, day_eff)
        loading, factors, unit_eff, day_eff = solve(reduce_all(shape, part), centred, mean)
    owned = lax.dynamic_slice_in_dim(factors, lax.axis_index(AXES) * slice_days, slice_days, 1)
    return (loading, owned, unit_eff[:, 0], day_eff[0])


def solution(mesh):
    return jax.shard_map(
        functools.partial(body, dict(mesh.shape)),
        mesh=mesh,
        in_specs=(P(AXES, None), P(AXES), P(None, AXES), P(None, AXES), P(AXES), P()),
        out_specs=(P(None, AXES), P(None, AXES), P(AXES), P()),
        check_vma=False,
    )
```

profile of v0, /device:TPU:1, one launch (start us, length us, event | category | flops | bytes accessed | tf_op | source)
XLA Modules:
  0.0 136.4 jit_solution(6254223505193599300)
XLA Ops:
  0.6 0.0 copy-start
  0.6 1.5 %copy.12.treat_ref = s32[256,1]{1,0:T(8,128)} copy(s32[256,1]{0,1:T(1,128)} %bitcast.13) | data formatting | bytes 2048 | tf_op jit(solution)/shard_map/broadcast_in_dim | solution.py:338
  2.1 18.1 %gather_days.1.fac_ref = f32[64,4096]{1,0:T(8,128)} custom-call(f32[64,128]{1,0:T(8,128)} %own_ref.1), custom_call_target="tpu_custom_call" | custom-call | tf_op jit(solution)/shard_map/gather_days/pallas_call | solution.py:137
  20.2 0.0 copy-done
  20.2 0.8 copy.11.unit_ref
  21.0 9.5 %impute.2 = (f32[288,8,128]{2,1,0:T(8,128)}, f32[256,4096]{1,0:T(8,128)}, f32[256,1]{1,0:T(8,128)}) custom-call(f32[256,4096]{1,0:T(8,128)} %panel_ref.3, s32[256,1]{1,0:T(8,128)} %copy.12.treat_ref, f32[64,256]{1,0:T(8,128)} %load_ref.1, f32[64,4096]{1,0:T(8,128)} %gather_days.1.fac_ref, f32[256,1]{1,0:T(8,128)} %copy.11.unit_ref, f32[1,4096]{1,0:T(1,128)} %bitcast.12), custom_call_target="tpu_custom_call" | custom-call | tf_op jit(solution)/shard_map/impute/pallas_call | solution.py:342
  30.5 28.7 %reduce_all.2 = f32[3,2,4,4,3,8,128]{6,5,4,3,2,1,0:T(8,128)} custom-call(f32[3,2,4,4,3,8,128]{6,5,4,3,2,1,0:T(8,128)} %bitcast.11), custom_call_target="tpu_custom_call" | custom-call | tf_op jit(solution)/shard_map/reduce_all/pallas_call | solution.py:158
  59.3 18.6 %solve.2 = (f32[64,256]{1,0:T(8,128)}, f32[64,4096]{1,0:T(8,128)}, f32[256,1]{1,0:T(8,128)}, f32[1,4096]{1,0:T(1,128)}) custom-call(f32[288,8,128]{2,1,0:T(8,128)} %bitcast.8, f32[256,4096]{1,0:T(8,128)} %get-tuple-element.19.cent_ref, f32[256,1]{1,0:T(8,128)} %get-tuple-element.20.mean_ref), custom_call_target="tpu_custom_call" | custom-call | tf_op jit(solution)/shard_map/solve/pallas_call | solution.py:343
  77.8 9.5 %impute.3 = (f32[288,8,128]{2,1,0:T(8,128)}, f32[256,4096]{1,0:T(8,128)}, f32[256,1]{1,0:T(8,128)}) custom-call(f32[256,4096]{1,0:T(8,128)} %panel_ref.3, s32[256,1]{1,0:T(8,128)} %copy.12.treat_ref, f32[64,256]{1,0:T(8,128)} %get-tuple-element.21.load_ref, f32[64,4096]{1,0:T(8,128)} %get-tuple-element.22.fac_ref, f32[256,1]{1,0:T(8,128)} %get-tuple-element.23.unit_ref, ...), custom_call_target="tpu_custom_call" | custom-call | tf_op jit(solution)/shard_map/impute/pallas_call | solution.py:342
  87.4 27.5 %reduce_all.3 = f32[3,2,4,4,3,8,128]{6,5,4,3,2,1,0:T(8,128)} custom-call(f32[3,2,4,4,3,8,128]{6,5,4,3,2,1,0:T(8,128)} %bitcast.10), custom_call_target="tpu_custom_call" | custom-call | tf_op jit(solution)/shard_map/reduce_all/pallas_call | solution.py:158
  114.9 18.6 %solve.3 = (f32[64,256]{1,0:T(8,128)}, f32[64,4096]{1,0:T(8,128)}, f32[256,1]{1,0:T(8,128)}, f32[1,4096]{1,0:T(1,128)}) custom-call(f32[288,8,128]{2,1,0:T(8,128)} %bitcast.9, f32[256,4096]{1,0:T(8,128)} %get-tuple-element.26.cent_ref, f32[256,1]{1,0:T(8,128)} %get-tuple-element.27.mean_ref), custom_call_target="tpu_custom_call" | custom-call | tf_op jit(solution)/shard_map/solve/pallas_call | solution.py:343
  133.5 1.4 %constant_dynamic-slice_fusion = f32[64,128]{1,0:T(8,128)} fusion(f32[64,4096]{1,0:T(8,128)} %get-tuple-element.29, s32[]{:T(128)S(6)} %select_n.3), kind=kLoop, calls=%fused_computation | loop fusion | bytes 65540 | tf_op jit(solution)/shard_map/dynamic_slice | solution.py:344
  134.9 1.6 %reduce = f32[256]{0:T(256)} reduce(f32[256,1]{1,0:T(8,128)} %get-tuple-element.30, f32[]{:T(128)} %constant.21), dimensions={1}, to_apply=%get-tuple-element.30.reduce_sub_computation | reduce | bytes 2052 | tf_op jit(solution)/shard_map/solve/pallas_call | solution.py:343
Async XLA Ops:
  0.6 19.6 %copy-start = (f32[256]{0:T(256)S(1)}, f32[256]{0:T(256)}, u32[]{:S(2)}) copy-start(f32[256]{0:T(256)} %param.10) | copy-start | bytes 3076
where the time goes:
time: 137 us; the launch traced here: 136 us
  Pallas kernels  131 us (96%)
  local copies, waits for them, and re-layouts  3.65 us (3%)
  other arithmetic  1.58 us (1%)
    pallas_call x2, Pallas kernels, reduce_all(): pl.pallas_call(functools.partial(reduce_kernel, shape), out_shape=jax.Sha...  56.3 us
    pallas_call x2, Pallas kernels, body(): solve(reduce_all(shape, part), centred, mean)  37.2 us
    pallas_call x2, Pallas kernels, body(): impute(panel, treat, loading, factors, unit_eff, day_eff)  19.1 us
    pallas_call x1, Pallas kernels, gather(): pl.pallas_call(functools.partial(gather_kernel, shape), out_shape=jax.Sha...  18.1 us

commit v1 on v0

v1 whole, which is shorter than its diff:
```python
import functools

import jax
import jax.numpy as jnp
from jax import lax
from jax.experimental import pallas as pl
from jax.experimental.pallas import tpu as pltpu
from jax.sharding import PartitionSpec as P

SWEEPS = 2
RIDGE = 1.0
WIDTH = 512
LANES = 128
AXES = ("gx", "gy", "gz")
MESH = pl.DeviceIdType.MESH
VMEM = pl.BlockSpec(memory_space=pltpu.VMEM)
ANY = pl.BlockSpec(memory_space=pl.ANY)
F32 = jnp.float32
BF16 = jnp.bfloat16


def mul(left, right, at):
    return lax.dot_general(left, right, ((at[:1], at[1:]), ((), ())), preferred_element_type=F32)


def halves(value):
    high = value.astype(BF16)
    return high, (value - high.astype(F32)).astype(BF16)


def wide_left(value):
    high, low = halves(value)
    return jnp.concatenate([high, high, low], 1)


def wide_right(value):
    high, low = halves(value)
    return jnp.concatenate([high, low, high], 0)


def quadrants(value, rows, cols):
    top = value[:rows, :cols] + value[:rows, cols:2 * cols]
    return top + (value[rows:, :cols] + value[rows:, cols:2 * cols])


def eye(rank):
    return lax.broadcasted_iota(jnp.int32, (rank, rank), 0) == lax.broadcasted_iota(jnp.int32, (rank, rank), 1)


def with_identity(matrix):
    unit = jnp.where(eye(matrix.shape[0]), 1.0, 0.0)
    return jnp.concatenate([matrix + RIDGE * unit, unit], 1)


def eliminate(work, first, last):
    row_at = lax.broadcasted_iota(jnp.int32, work.shape, 0)
    for k in range(first, last):
        pivot_row = work[k:k + 1, :] * (1.0 / work[k:k + 1, k:k + 1])
        work = jnp.where(row_at == k, pivot_row, work - work[:, k:k + 1] * pivot_row)
    return work


def column(row, rank):
    return jnp.sum(jnp.where(eye(rank), row, 0.0), 1, keepdims=True)


class Links:
    def __init__(self, shape, send, recv):
        self.shape, self.send, self.recv = shape, send, recv
        self.here = {axis: lax.axis_index(axis) for axis in AXES}
        self.index, self.open = 0, []

    def at(self, axis, step):
        return lax.rem(self.here[axis] + step, self.shape[axis])

    def device(self, axis, step):
        place = dict(self.here)
        place[axis] = self.at(axis, step)
        return tuple(place[name] for name in AXES)

    def steps(self, axis):
        return range(1, self.shape[axis])

    def meet(self):
        barrier = pltpu.get_barrier_semaphore()
        count = 0
        for axis in AXES:
            for step in self.steps(axis):
                pl.semaphore_signal(barrier, inc=1, device_id=self.device(axis, step), device_id_type=MESH)
                count += 1
        pl.semaphore_wait(barrier, count)

    def copy(self, source, target, axis, step):
        copy = pltpu.make_async_remote_copy(
            source, target, self.send.at[self.index], self.recv.at[self.index],
            device_id=self.device(axis, step), device_id_type=MESH)
        self.index += 1
        copy.start()
        self.open.append(copy)
        return copy

    def settle(self):
        for copy in self.open:
            copy.wait_send()
        self.open = []


def arrive(copies):
    for copy in copies:
        copy.wait_recv()


class SmallSum:
    order = ("gz", "gy", "gx")

    def __init__(self, links, mine, hold):
        self.links, self.mine, self.hold = links, mine, hold
        self.stage, self.slot, self.moving = 0, 0, []

    def start(self, value):
        axis = self.order[self.stage]
        mine = self.mine.at[self.stage]
        mine[...] = value
        self.value = value
        self.first = self.slot
        self.moving = []
        for step in self.links.steps(axis):
            self.moving.append(self.links.copy(mine, self.hold.at[self.slot], axis, step))
            self.slot += 1

    def finish(self):
        arrive(self.moving)
        value = self.mine[self.stage]
        for slot in range(self.first, self.slot):
            value = value + self.hold[slot]
        self.stage += 1
        return value

    def step(self):
        self.start(self.finish())


def kernel(shape, panel_ref, treat_ref, load_ref, fac_ref, unit_ref, day_ref,
           load_out, fac_out, unit_out, day_out,
           pan, xh, xl, blocks, fh, fl, bd, part, hold_z, hold_y, hold_x, sum_z, sum_y,
           gram_mine, gram_hold, tail_mine, tail_hold, lt, lw, ls, limit, ub, rsum, local, send, recv):
    nx, ny, nz = (shape[axis] for axis in AXES)
    devices = nx * ny * nz
    units, days = panel_ref.shape
    rank, w = fac_ref.shape
    chunk = days // nx
    width = min(WIDTH, chunk)
    per = width // w
    total_units = units * devices
    fold = LANES // rank
    links = Links(shape, send, recv)
    x, y, z = (links.here[axis] for axis in AXES)

    def fetch(at):
        return pltpu.make_async_copy(
            panel_ref.at[:, pl.ds(pl.multiple_of(at * chunk, chunk), chunk)], pan.at[at], local.at[at])

    for c in range(nx):
        fetch(c).start()
    blocks[0, x, y, z, 0:rank, :] = fac_ref[...]
    links.meet()

    def gather(buf, consume):
        own = buf.at[x, y, z]
        xs = [links.copy(own, own, "gx", step) for step in links.steps("gx")]
        ys, zs = [], []

        def spread(i):
            block = buf.at[lax.rem(x + nx - i, nx), y, z]
            ys.append([links.copy(block, block, "gy", step) for step in links.steps("gy")])

        def pair(i):
            arrive(ys[i])
            line = buf.at[lax.rem(x + nx - i, nx), :, z]
            zs.append([links.copy(line, line, "gz", step) for step in links.steps("gz")])

        spread(0)
        for i in range(1, nx):
            arrive(xs[i - 1:i])
            spread(i)
        pair(0)
        for i in range(nx):
            if i + 1 < nx:
                pair(i + 1)
            arrive(zs[i])
            consume(i, lax.rem(x + nx - i, nx))

    def take(buf, at):
        for j in range(ny):
            for k in range(nz):
                c = (j * nz + k) * w
                high, low = halves(buf[at, j, k, 0:rank, :])
                fh[at, :, c:c + w] = high
                fl[at, :, c:c + w] = low

    load = load_ref[...]
    flip = jnp.broadcast_to(unit_ref[...], (LANES, units)).T
    ub[...] = flip
    lane = lax.broadcasted_iota(jnp.int32, (units, LANES), 1).astype(F32)
    limit[...] = jnp.broadcast_to(treat_ref[...].astype(F32), (LANES, units)).T - lane
    for c in range(nx):
        bd[c] = day_ref[:, c * chunk:(c + 1) * chunk]
    row_at = lax.broadcasted_iota(jnp.int32, (8, LANES), 0)
    pad = jnp.zeros((8, LANES - rank), F32)

    def impute(at):
        def tile(t, _):
            start = pl.multiple_of(t * width, width)
            cols = pl.ds(start, width)
            high, low = fh[at, :, cols], fl[at, :, cols]
            fitted = mul(lw[...], jnp.concatenate([high, low, high], 0), (1, 0))
            first = (at * chunk + start).astype(F32)
            day = bd[at, :, cols]
            es, xs = [], []
            for c in range(width // LANES):
                span = slice(c * LANES, (c + 1) * LANES)
                fit = fitted[:, span]
                base = ub[...] + day[:, span]
                miss = pan[at, :, pl.ds(pl.multiple_of(start + c * LANES, LANES), LANES)] - base - fit
                e = jnp.where(limit[...] > first + float(c * LANES), miss, 0.0)
                es.append(e)
                xs.append(e + fit)
            total = es[0]
            for e in es[1:]:
                total = total + e
            rsum[...] += total
            sums = jnp.sum(jnp.concatenate(es, 1), 0, keepdims=True)
            xhigh, xlow = halves(jnp.concatenate(xs, 1))
            xh[at, :, cols] = xhigh
            xl[at, :, cols] = xlow
            both = mul(ls[...], xhigh, (1, 0))
            out = both[:rank] + both[rank:] + mul(ls[0:rank, :], xlow, (1, 0))
            for c in range(per):
                place = t * per + c
                span = slice(c * w, (c + 1) * w)
                spot = (at, lax.rem(place, nz), lax.div(place, nz))
                part[spot + (slice(0, rank),)] = out[:, span]
                part[spot + (slice(rank, rank + 8),)] = jnp.where(row_at[:, :w] == 0, sums[:, span], 0.0)
            return 0

        lax.fori_loop(0, chunk // width, tile, 0)

    for sweep in range(SWEEPS):
        if sweep == 0:
            lt[...] = load.T
        turned = lt[...]
        lw[...] = wide_left(turned)
        high, low = halves(load)
        stack = jnp.concatenate([high, low], 0)
        ls[...] = stack
        gram = quadrants(mul(stack, stack, (1, 1)), rank, rank)
        each = rank // fold
        packed = jnp.concatenate([gram[f * each:(f + 1) * each] for f in range(fold)], 1)
        load_sum = jnp.sum(turned, 0, keepdims=True)
        load_sum = jnp.concatenate([load_sum, jnp.zeros((1, LANES - rank), F32)], 1) if rank < LANES else load_sum
        unit_sum = jnp.sum(ub[:, 0:1], 0, keepdims=True)
        extra = jnp.where(row_at == 0, load_sum, jnp.where(row_at == 1, unit_sum, 0.0))
        grams = SmallSum(links, gram_mine.at[sweep], gram_hold.at[sweep])
        grams.start(jnp.concatenate([packed, extra], 0))
        rsum[...] = jnp.zeros_like(rsum)
        hz, hy, hx = hold_z.at[sweep], hold_y.at[sweep], hold_x.at[sweep]
        pieces = []

        def give(at):
            pieces.append({"at": at, "z": [
                links.copy(part.at[at, links.at("gz", step)], hz.at[step - 1, at], "gz", step)
                for step in links.steps("gz")]})

        def across(n):
            piece = pieces[n]
            at = piece["at"]
            arrive(piece["z"])
            value = part[at, z]
            for slot in range(nz - 1):
                value = value + hz[slot, at]
            sum_z[at] = value
            piece["y"] = [
                links.copy(sum_z.at[at, links.at("gy", step)], hy.at[step - 1, at], "gy", step)
                for step in links.steps("gy")]

        def along(n, offset):
            piece = pieces[n]
            at = piece["at"]
            arrive(piece["y"])
            value = sum_z[at, y]
            for slot in range(ny - 1):
                value = value + hy[slot, at]
            sum_y[at] = value
            piece["x"] = [links.copy(sum_y.at[at], hx.at[offset - 1], "gx", offset)] if offset else []

        offsets = [(nx - i) % nx for i in range(nx)] if sweep == 0 else [(i + 1) % nx for i in range(nx)]

        def chunk_step(n, at):
            if sweep == 0:
                fetch(at).wait()
            impute(at)
            give(at)
            if n >= 1:
                across(n - 1)
            if n >= 2:
                along(n - 2, offsets[n - 2])
            if n < 2:
                grams.step()

        if sweep == 0:
            def begin(i, at):
                take(blocks.at[0], at)
                chunk_step(i, at)

            gather(blocks.at[0], begin)
        else:
            for n in range(nx):
                chunk_step(n, lax.rem(x + offsets[n], nx))

        rows = jnp.sum(rsum[...], 1, keepdims=True)
        weighted_rows = jnp.sum(turned * rows, 0, keepdims=True)
        if rank < LANES:
            weighted_rows = jnp.concatenate([weighted_rows, jnp.zeros((1, LANES - rank), F32)], 1)
        row_total = jnp.sum(rows, 0, keepdims=True)
        tails = SmallSum(links, tail_mine.at[sweep], tail_hold.at[sweep])
        tails.start(jnp.where(row_at == 0, weighted_rows, jnp.where(row_at == 1, row_total, 0.0)))
        gram_all = grams.finish()
        across(nx - 1)
        along(nx - 2, offsets[nx - 2])
        tails.step()
        work = jnp.concatenate([gram_all[0:each, f * rank:(f + 1) * rank] for f in range(fold)], 0)
        work = eliminate(with_identity(work), 0, rank // 2)
        along(nx - 1, offsets[nx - 1])
        tails.step()
        inverse = wide_left(eliminate(work, rank // 2, rank)[:, rank:])
        tail_all = tails.finish()
        for piece in pieces:
            arrive(piece["x"])
        value = sum_y[x]
        for slot in range(nx - 1):
            value = value + hx[slot]
        sum_l = column(gram_all[each:each + 1, 0:rank], rank)
        old_units = gram_all[each + 1:each + 2, 0:1] / total_units
        sum_lr = column(tail_all[0:1, 0:rank], rank)
        mean = tail_all[1:2, 0:1] / (total_units * days)
        old_days = sum(jnp.sum(bd[c], 1, keepdims=True) for c in range(nx)) / days
        moved = value[rank:rank + 1, :] / total_units - (mean + old_days)
        shift = (mean + old_units) - moved
        factors = mul(inverse, wide_right(value[0:rank, :] - sum_lr / days + sum_l * shift), (1, 0))
        own = blocks.at[sweep + 1, x, y, z]
        own[0:rank, :] = factors
        own[rank:rank + 8, :] = jnp.where(row_at[:, :w] == 0, moved, 0.0)
        if sweep == SWEEPS - 1:
            fac_out[...] = factors
        delta = rows / days - (mean + old_units)
        buf = blocks.at[sweep + 1]
        sums = {"square": None, "project": None, "plain": None, "days": None}

        def keep(name, value):
            sums[name] = value if sums[name] is None else sums[name] + value

        def project(i, at):
            take(buf, at)
            both = jnp.concatenate([fh[at], fl[at]], 0)
            keep("square", mul(both, both, (1, 1)))
            keep("project", mul(xh[at], both, (1, 1)) + mul(xl[at], both, (1, 1)))
            for j in range(ny):
                for k in range(nz):
                    c = (j * nz + k) * w
                    change = buf[at, j, k, rank:rank + 1, :]
                    block = buf[at, j, k, 0:rank, :]
                    keep("plain", block)
                    keep("days", block * change)
                    bd[at, :, c:c + w] = bd[at, :, c:c + w] + change

        gather(buf, project)
        work = eliminate(with_identity(quadrants(sums["square"], rank, rank)), 0, rank)
        day_term = jnp.sum(sums["days"], 1, keepdims=True)
        plain = jnp.sum(sums["plain"], 1, keepdims=True)
        day_row = jnp.sum(jnp.where(eye(rank), day_term, 0.0), 0, keepdims=True)
        plain_row = jnp.sum(jnp.where(eye(rank), plain, 0.0), 0, keepdims=True)
        project_all = sums["project"][:, :rank] + sums["project"][:, rank:]
        project_all = project_all - delta * plain_row - day_row
        turned = mul(wide_left(project_all), wide_right(work[:, rank:]), (1, 0))
        lt[...] = turned
        load = turned.T
        ub[...] = ub[...] + delta
        links.settle()

    load_out[...] = load
    unit_out[...] = ub[...].T[0:1, :]
    for c in range(nx):
        day_out[:, c * chunk:(c + 1) * chunk] = bd[c]


def body(shape, panel, treat_start, loading_init, factor_init, unit_init, day_init):
    units, days = panel.shape
    rank, w = factor_init.shape
    nx, ny, nz = (shape[axis] for axis in AXES)
    chunk = days // nx
    high = rank + 8
    each = rank * rank // LANES + 8
    peers = nx + ny + nz - 3
    count = SWEEPS * (2 * peers + nx * (ny + nz - 2) + nx - 1) + (SWEEPS + 1) * (nx - 1 + nx * (ny + nz - 2))
    dma = pltpu.SemaphoreType.DMA

    def array(*sizes):
        return jax.ShapeDtypeStruct(sizes, F32)

    loading, factors, unit_eff, day_eff = pl.pallas_call(
        functools.partial(kernel, shape),
        out_shape=(array(rank, units), array(rank, w), array(1, units), array(1, days)),
        in_specs=[ANY] + [VMEM] * 5,
        out_specs=(VMEM,) * 4,
        scratch_shapes=[
            pltpu.VMEM((nx, units, chunk), F32),
            pltpu.VMEM((nx, units, chunk), BF16),
            pltpu.VMEM((nx, units, chunk), BF16),
            pltpu.VMEM((SWEEPS + 1, nx, ny, nz, high, w), F32),
            pltpu.VMEM((nx, rank, chunk), BF16),
            pltpu.VMEM((nx, rank, chunk), BF16),
            pltpu.VMEM((nx, 1, chunk), F32),
            pltpu.VMEM((nx, nz, ny, high, w), F32),
            pltpu.VMEM((SWEEPS, nz - 1, nx, ny, high, w), F32),
            pltpu.VMEM((SWEEPS, ny - 1, nx, high, w), F32),
            pltpu.VMEM((SWEEPS, nx - 1, high, w), F32),
            pltpu.VMEM((nx, ny, high, w), F32),
            pltpu.VMEM((nx, high, w), F32),
            pltpu.VMEM((SWEEPS, 3, each, LANES), F32),
            pltpu.VMEM((SWEEPS, peers, each, LANES), F32),
            pltpu.VMEM((SWEEPS, 3, 8, LANES), F32),
            pltpu.VMEM((SWEEPS, peers, 8, LANES), F32),
            pltpu.VMEM((units, rank), F32),
            pltpu.VMEM((units, 3 * rank), BF16),
            pltpu.VMEM((2 * rank, units), BF16),
            pltpu.VMEM((units, LANES), F32),
            pltpu.VMEM((units, LANES), F32),
            pltpu.VMEM((units, LANES), F32),
            dma((nx,)),
            dma((count,)),
            dma((count,)),
        ],
        compiler_params=pltpu.CompilerParams(collective_id=0, has_side_effects=True, vmem_limit_bytes=60 * 1024 * 1024),
        name="sweeps",
    )(panel, treat_start[None, :], loading_init, factor_init, unit_init[None, :], day_init[None, :])
    return (loading, factors, unit_eff[0], day_eff[0])


def solution(mesh):
    return jax.shard_map(
        functools.partial(body, dict(mesh.shape)),
        mesh=mesh,
        in_specs=(P(AXES, None), P(AXES), P(None, AXES), P(None, AXES), P(AXES), P()),
        out_specs=(P(None, AXES), P(None, AXES), P(AXES), P()),
        check_vma=False,
    )
```

time: 137 us -> 105 us (0.77)
  Pallas kernels: 131 us -> 98 us
  local copies, waits for them, and re-layouts: 3.65 us -> 5.39 us
  other arithmetic: 1.58 us -> 0 us
    pallas_call x7 -> x1, Pallas kernels: 131 us -> 98 us  [body(): pl.pallas_call(functools.partial(kernel, shape), out_shape=(array(rank, u...]
    unnamed x2 -> x4, local copies, waits for them, and re-layouts: 0.01 us -> 5.39 us
    broadcast_in_dim x2 -> x0, local copies, waits for them, and re-layouts: 2.27 us -> none  [the longest x1 1.47 us: body(): treat = treat_start[:, None]]
    pallas_call x1 -> x0, other arithmetic: 1.58 us -> none  [body(): solve(reduce_all(shape, part), centred, mean)]
    dynamic_slice x1 -> x0, local copies, waits for them, and re-layouts: 1.37 us -> none  [body(): lax.dynamic_slice_in_dim(factors, lax.axis_index(AXES) * slice_days, slic...]
where the time goes in v1:
time: 105 us; the launch traced here: 104 us
  Pallas kernels  98 us (93%)
  local copies, waits for them, and re-layouts  5.39 us (5%)
    pallas_call x1, Pallas kernels, body(): pl.pallas_call(functools.partial(kernel, shape), out_shape=(array(rank, u...  98 us
    unnamed x4, local copies, waits for them, and re-layouts  5.39 us

profile of v1, /device:TPU:1, one launch (start us, length us, event | category | flops | bytes accessed | tf_op | source)
XLA Modules:
  0.0 104.1 jit_solution(16980962355663979354)
XLA Ops:
  0.6 98.0 %sweeps.1 = (f32[64,256]{1,0:T(8,128)}, f32[64,128]{1,0:T(8,128)}, f32[1,256]{1,0:T(1,128)}, f32[1,4096]{1,0:T(1,128)}) custom-call(f32[256,4096]{1,0:T(8,128)} %panel_ref.1, s32[1,256]{1,0:T(1,128)} %bitcast.8, f32[64,256]{1,0:T(8,128)} %load_ref.1, f32[64,128]{1,0:T(8,128)} %fac_ref.1, f32[1,256]{1,0:T(1,128)} %bitcast.9, f32[1,4096]{1,0:T(1,128)} %bitcast.5), custom_call_target="tpu_custom_call" | custom-call | tf_op jit(solution)/shard_map/sweeps/pallas_call | solution.py:410
  98.7 1.5 %copy.14 = f32[64,256]{1,0:T(8,128)} copy(f32[64,256]{1,0:T(8,128)} %get-tuple-element.16) | data formatting | bytes 131072
  100.1 1.4 %copy.15 = f32[64,128]{1,0:T(8,128)} copy(f32[64,128]{1,0:T(8,128)} %get-tuple-element.17) | data formatting | bytes 65536
  101.5 1.2 %copy.16 = f32[256]{0:T(256)} copy(f32[256]{0:T(256)} %bitcast.7) | data formatting | bytes 2048
  102.7 1.3 %copy.17 = f32[4096]{0:T(1024)} copy(f32[4096]{0:T(1024)} %bitcast.6) | data formatting | bytes 32768

commit v2 on v1

v2 whole, which is shorter than its diff:
```python
import functools

import jax
import jax.numpy as jnp
from jax import lax
from jax.experimental import pallas as pl
from jax.experimental.pallas import tpu as pltpu
from jax.sharding import PartitionSpec as P

SWEEPS = 2
RIDGE = 1.0
WIDTH = 512
LANES = 128
AXES = ("gx", "gy", "gz")
MESH = pl.DeviceIdType.MESH
VMEM = pl.BlockSpec(memory_space=pltpu.VMEM)
ANY = pl.BlockSpec(memory_space=pl.ANY)
F32 = jnp.float32
BF16 = jnp.bfloat16


def mul(left, right, at):
    return lax.dot_general(left, right, ((at[:1], at[1:]), ((), ())), preferred_element_type=F32)


def halves(value):
    high = value.astype(BF16)
    return high, (value - high.astype(F32)).astype(BF16)


def wide_left(value):
    high, low = halves(value)
    return jnp.concatenate([high, high, low], 1)


def wide_right(value):
    high, low = halves(value)
    return jnp.concatenate([high, low, high], 0)


def quadrants(value, rows, cols):
    top = value[:rows, :cols] + value[:rows, cols:2 * cols]
    return top + (value[rows:, :cols] + value[rows:, cols:2 * cols])


def eye(rank):
    return lax.broadcasted_iota(jnp.int32, (rank, rank), 0) == lax.broadcasted_iota(jnp.int32, (rank, rank), 1)


def with_identity(matrix):
    unit = jnp.where(eye(matrix.shape[0]), 1.0, 0.0)
    return jnp.concatenate([matrix + RIDGE * unit, unit], 1)


def pair_inverse(a, b, c, d):
    scale = 1.0 / (a * d - b * c)
    return ((d * scale, -(b * scale)), (-(c * scale), a * scale))


def product(left, right):
    return [[left[i][0] * right[0][j] + left[i][1] * right[1][j] for j in range(2)] for i in range(2)]


def quad_inverse(m):
    first = pair_inverse(m[0][0], m[0][1], m[1][0], m[1][1])
    upper = product(first, [m[0][2:], m[1][2:]])
    lower = product([m[2][:2], m[3][:2]], first)
    inner = product([m[2][:2], m[3][:2]], upper)
    last = pair_inverse(*(m[2 + i][2 + j] - inner[i][j] for i in range(2) for j in range(2)))
    right = product(upper, last)
    left = product(last, lower)
    more = product(right, lower)
    return [[first[i][0] + more[i][0], first[i][1] + more[i][1], -right[i][0], -right[i][1]] for i in range(2)] + [
        [-left[i][0], -left[i][1], last[i][0], last[i][1]] for i in range(2)]


def eliminate(work, first, last):
    row_at = lax.broadcasted_iota(jnp.int32, work.shape, 0)
    for k in range(4 * first, 4 * last, 4):
        cols = [jnp.broadcast_to(work[:, k + i:k + i + 1], work.shape) for i in range(4)]
        rows = [work[k + i:k + i + 1] for i in range(4)]
        block = quad_inverse([[cols[j][k + i:k + i + 1] for j in range(4)] for i in range(4)])
        pivots = [(b[0] * rows[0] + b[1] * rows[1]) + (b[2] * rows[2] + b[3] * rows[3]) for b in block]
        work = work - (cols[0] * pivots[0] + cols[1] * pivots[1]) - (cols[2] * pivots[2] + cols[3] * pivots[3])
        for i in range(4):
            work = jnp.where(row_at == k + i, pivots[i], work)
    return work


def column(row, rank):
    return jnp.sum(jnp.where(eye(rank), row, 0.0), 1, keepdims=True)


def nearest(here, count):
    lists = [sorted(range(count), key=lambda at: (abs(at - place), at)) for place in range(count)]
    found = []
    for rank in range(count):
        value = lists[0][rank]
        for place in range(1, count):
            value = jnp.where(here == place, lists[place][rank], value)
        found.append(value)
    return found


class Exchange:
    def __init__(self, links, axis, order, source, target):
        self.links, self.axis, self.target = links, axis, target
        self.base = links.take(links.shape[axis])
        for slot, there in enumerate(order):
            copy = self.copy(source(there), links.here[axis], there, slot)
            copy.start()
            links.open.append(copy)

    def copy(self, source, place, there, slot):
        links = self.links
        return pltpu.make_async_remote_copy(
            source, self.target(place), links.send.at[self.base + slot], links.recv.at[self.base + place],
            device_id=links.device(self.axis, there), device_id_type=MESH)

    def wait(self, *places):
        for place in places:
            self.copy(self.target(place), place, place, 0).wait_recv()


class Links:
    def __init__(self, shape, send, recv):
        self.shape, self.send, self.recv = shape, send, recv
        self.here = {axis: lax.axis_index(axis) for axis in AXES}
        self.others = {
            axis: [lax.rem(self.here[axis] + step, shape[axis]) for step in range(1, shape[axis])] for axis in AXES}
        self.index, self.open = 0, []

    def take(self, count):
        self.index += count
        return self.index - count

    def device(self, axis, there):
        return tuple(there if name == axis else self.here[name] for name in AXES)

    def meet(self):
        barrier = pltpu.get_barrier_semaphore()
        count = 0
        for axis in AXES:
            for there in self.others[axis]:
                pl.semaphore_signal(barrier, inc=1, device_id=self.device(axis, there), device_id_type=MESH)
                count += 1
        pl.semaphore_wait(barrier, count)

    def settle(self):
        for copy in self.open:
            copy.wait_send()
        self.open = []


class SmallSum:
    order = ("gz", "gy", "gx")

    def __init__(self, links, hold, value):
        self.links, self.hold, self.stage, self.slot = links, hold, 0, 0
        self.start(value)

    def start(self, value):
        links, axis, slot = self.links, self.order[self.stage], self.slot
        self.hold[slot + links.here[axis]] = value

        def spot(place):
            return self.hold.at[slot + place]

        self.moving = Exchange(links, axis, links.others[axis], lambda there: spot(links.here[axis]), spot)

    def finish(self):
        axis = self.order[self.stage]
        self.moving.wait(*self.links.others[axis])
        value = self.hold[self.slot]
        for place in range(1, self.links.shape[axis]):
            value = value + self.hold[self.slot + place]
        self.slot += self.links.shape[axis]
        self.stage += 1
        return value

    def step(self):
        self.start(self.finish())


def kernel(shape, panel_ref, treat_ref, load_ref, fac_ref, unit_ref, day_ref,
           load_out, fac_out, unit_out, day_out,
           pan, xh, xl, blocks, fh, fl, bd, part, hold_z, hold_y, hold_x, sum_z, sum_y,
           gram_hold, tail_hold, lt, lw, ls, limit, ub, rsum, local, send, recv):
    nx, ny, nz = (shape[axis] for axis in AXES)
    devices = nx * ny * nz
    units, days = panel_ref.shape
    rank, w = fac_ref.shape
    chunk = days // nx
    width = min(WIDTH, chunk)
    per = width // w
    total_units = units * devices
    fold = LANES // rank
    links = Links(shape, send, recv)
    x, y, z = (links.here[axis] for axis in AXES)

    def fetch(at):
        return pltpu.make_async_copy(
            panel_ref.at[:, pl.ds(pl.multiple_of(at * chunk, chunk), chunk)], pan.at[at], local.at[at])

    for c in range(nx):
        fetch(c).start()
    blocks[0, x, y, z, 0:rank, :] = fac_ref[...]
    links.meet()

    line = nearest(x, nx)

    def gather(buf, rows, consume):
        def spot(at, j):
            return buf.at[at, j, z, 0:rows] if rows < buf.shape[3] else buf.at[at, j, z]

        def pair_spot(at):
            return lambda k: buf.at[at, :, k, 0:rows] if rows < buf.shape[3] else buf.at[at, :, k]

        ys, zs = [], []

        def spread(at):
            ys.append(Exchange(links, "gy", links.others["gy"], lambda there: spot(at, y), lambda j: spot(at, j)))

        def pair(n):
            ys[n].wait(*links.others["gy"])
            place = pair_spot(line[n])
            zs.append(Exchange(links, "gz", links.others["gz"], lambda there: place(z), place))

        spread(x)
        xs = Exchange(links, "gx", line[1:], lambda there: spot(x, y), lambda i: spot(i, y))
        for at in line[1:]:
            xs.wait(at)
            spread(at)
        pair(0)
        for n in range(nx):
            if n + 1 < nx:
                pair(n + 1)
            zs[n].wait(*links.others["gz"])
            consume(n, line[n])

    def take(buf, at, shift):
        found = []
        for j in range(ny):
            for k in range(nz):
                c = (j * nz + k) * w
                block = buf[at, j, k, 0:rank, :]
                if shift is not None:
                    block = block + shift
                high, low = halves(block)
                fh[at, :, c:c + w] = high
                fl[at, :, c:c + w] = low
                found.append(block)
        return found

    load = load_ref[...]
    flip = jnp.broadcast_to(unit_ref[...], (LANES, units)).T
    ub[...] = flip
    lane = lax.broadcasted_iota(jnp.int32, (units, LANES), 1).astype(F32)
    limit[...] = jnp.broadcast_to(treat_ref[...].astype(F32), (LANES, units)).T - lane
    for c in range(nx):
        bd[c] = day_ref[:, c * chunk:(c + 1) * chunk]
    row_at = lax.broadcasted_iota(jnp.int32, (8, LANES), 0)
    pad = jnp.zeros((8, LANES - rank), F32)

    def impute(at):
        def tile(t, _):
            start = pl.multiple_of(t * width, width)
            cols = pl.ds(start, width)
            high, low = fh[at, :, cols], fl[at, :, cols]
            fitted = mul(lw[...], jnp.concatenate([high, low, high], 0), (1, 0))
            first = (at * chunk + start).astype(F32)
            day = bd[at, :, cols]
            es, xs = [], []
            for c in range(width // LANES):
                span = slice(c * LANES, (c + 1) * LANES)
                fit = fitted[:, span]
                base = ub[...] + day[:, span]
                miss = pan[at, :, pl.ds(pl.multiple_of(start + c * LANES, LANES), LANES)] - base - fit
                e = jnp.where(limit[...] > first + float(c * LANES), miss, 0.0)
                es.append(e)
                xs.append(e + fit)
            total = es[0]
            for e in es[1:]:
                total = total + e
            rsum[...] += total
            sums = jnp.sum(jnp.concatenate(es, 1), 0, keepdims=True)
            xhigh, xlow = halves(jnp.concatenate(xs, 1))
            xh[at, :, cols] = xhigh
            xl[at, :, cols] = xlow
            both = mul(ls[...], xhigh, (1, 0))
            out = both[:rank] + both[rank:] + mul(ls[0:rank, :], xlow, (1, 0))
            for c in range(per):
                place = t * per + c
                span = slice(c * w, (c + 1) * w)
                spot = (at, lax.rem(place, nz), lax.div(place, nz))
                part[spot + (slice(0, rank),)] = out[:, span]
                part[spot + (slice(rank, rank + 1),)] = sums[:, span]
            return 0

        lax.fori_loop(0, chunk // width, tile, 0)

    for sweep in range(SWEEPS):
        if sweep == 0:
            lt[...] = load.T
        turned = lt[...]
        lw[...] = wide_left(turned)
        high, low = halves(load)
        stack = jnp.concatenate([high, low], 0)
        ls[...] = stack
        gram = quadrants(mul(stack, stack, (1, 1)), rank, rank)
        each = rank // fold
        packed = jnp.concatenate([gram[f * each:(f + 1) * each] for f in range(fold)], 1)
        load_sum = jnp.sum(turned, 0, keepdims=True)
        load_sum = jnp.concatenate([load_sum, jnp.zeros((1, LANES - rank), F32)], 1) if rank < LANES else load_sum
        unit_sum = jnp.sum(ub[:, 0:1], 0, keepdims=True)
        extra = jnp.where(row_at == 0, load_sum, jnp.where(row_at == 1, unit_sum, 0.0))
        grams = SmallSum(links, gram_hold.at[sweep], jnp.concatenate([packed, extra], 0))
        rsum[...] = jnp.zeros_like(rsum)
        hz, hy, hx = hold_z.at[sweep], hold_y.at[sweep], hold_x.at[sweep]
        order = line if sweep == 0 else line[:0:-1] + line[:1]
        by_z, by_y, by_x = [], [], []

        def give(n):
            at = order[n]
            by_z.append(Exchange(
                links, "gz", links.others["gz"], lambda there: part.at[at, there], lambda k: hz.at[k, at]))

        def across(n):
            at = order[n]
            by_z[n].wait(*links.others["gz"])
            value = part[at, z]
            for k in links.others["gz"]:
                value = value + hz[k, at]
            sum_z[at] = value
            by_y.append(Exchange(
                links, "gy", links.others["gy"], lambda there: sum_z.at[at, there], lambda j: hy.at[j, at]))

        def along(n):
            at = order[n]
            by_y[n].wait(*links.others["gy"])
            value = sum_z[at, y]
            for j in links.others["gy"]:
                value = value + hy[j, at]
            sum_y[at] = value

        def forward(n):
            at = order[n]
            copy = pltpu.make_async_remote_copy(
                sum_y.at[at], hx.at[x], send.at[last_base + n], recv.at[last_base + x],
                device_id=links.device("gx", at), device_id_type=MESH)
            copy.start()
            links.open.append(copy)

        last_base = links.take(nx)
        local_piece = 0 if sweep == 0 else nx - 1

        def chunk_step(n):
            if sweep == 0:
                fetch(order[n]).wait()
            impute(order[n])
            give(n)
            if n >= 1:
                across(n - 1)
            if n == 0:
                grams.step()

        if sweep == 0:
            def begin(n, at):
                take(blocks.at[0], at, None)
                chunk_step(n)

            gather(blocks.at[0], rank, begin)
        else:
            for n in range(nx):
                chunk_step(n)

        rows = jnp.sum(rsum[...], 1, keepdims=True)
        weighted_rows = jnp.sum(turned * rows, 0, keepdims=True)
        if rank < LANES:
            weighted_rows = jnp.concatenate([weighted_rows, jnp.zeros((1, LANES - rank), F32)], 1)
        row_total = jnp.sum(rows, 0, keepdims=True)
        tails = SmallSum(
            links, tail_hold.at[sweep], jnp.where(row_at == 0, weighted_rows, jnp.where(row_at == 1, row_total, 0.0)))
        grams.step()
        across(nx - 1)
        tails.step()

        def pass_on(n):
            along(n)
            if n != local_piece:
                forward(n)

        for n in range(nx - 2):
            pass_on(n)
        gram_all = grams.finish()
        work = jnp.concatenate([gram_all[0:each, f * rank:(f + 1) * rank] for f in range(fold)], 0)
        work = eliminate(with_identity(work), 0, rank // 8)
        pass_on(nx - 2)
        tails.step()
        work = eliminate(work, rank // 8, rank // 4)
        pass_on(nx - 1)
        inverse = wide_left(work[:, rank:])
        sum_l = column(gram_all[each:each + 1, 0:rank], rank)
        old_units = gram_all[each + 1:each + 2, 0:1] / total_units
        old_days = sum(jnp.sum(bd[c], 1, keepdims=True) for c in range(nx)) / days
        for at in line[1:]:
            pltpu.make_async_remote_copy(
                hx.at[at], hx.at[at], send.at[last_base], recv.at[last_base + at],
                device_id=links.device("gx", at), device_id_type=MESH).wait_recv()
        value = sum_y[x]
        for at in line[1:]:
            value = value + hx[at]
        moved = value[rank:rank + 1, :] / total_units
        factors = mul(inverse, wide_right(value[0:rank, :] + sum_l * (old_units + old_days - moved)), (1, 0))
        own = blocks.at[sweep + 1, x, y, z]
        own[0:rank, :] = factors
        own[rank:rank + 1, :] = moved - old_days
        buf = blocks.at[sweep + 1]
        sums, after = {}, {}

        def keep(name, value):
            sums[name] = sums[name] + value if name in sums else value

        def project(n, at):
            if n == 0:
                tail_all = tails.finish()
                mean = tail_all[1:2, 0:1] / (total_units * days)
                right = sum_l * (2.0 * mean) - column(tail_all[0:1, 0:rank], rank) / days
                shift = mul(inverse, wide_right(jnp.broadcast_to(right, (rank, LANES))), (1, 0))[:, 0:1]
                after.update(mean=mean, shift=shift, delta=rows / days - (mean + old_units))
            found = take(buf, at, after["shift"])
            both = jnp.concatenate([fh[at], fl[at]], 0)
            keep("square", mul(both, both, (1, 1)))
            keep("project", mul(xh[at], both, (1, 1)) + mul(xl[at], both, (1, 1)))
            for j in range(ny):
                for k in range(nz):
                    c = (j * nz + k) * w
                    change = buf[at, j, k, rank:rank + 1, :] - after["mean"]
                    block = found[j * nz + k]
                    keep("plain", block)
                    keep("days", block * change)
                    bd[at, :, c:c + w] = bd[at, :, c:c + w] + change

        gather(buf, rank + 1, project)
        delta = after["delta"]
        work = eliminate(with_identity(quadrants(sums["square"], rank, rank)), 0, rank // 4)
        day_term = jnp.sum(sums["days"], 1, keepdims=True)
        plain = jnp.sum(sums["plain"], 1, keepdims=True)
        day_row = jnp.sum(jnp.where(eye(rank), day_term, 0.0), 0, keepdims=True)
        plain_row = jnp.sum(jnp.where(eye(rank), plain, 0.0), 0, keepdims=True)
        project_all = sums["project"][:, :rank] + sums["project"][:, rank:]
        project_all = project_all - delta * plain_row - day_row
        turned = mul(wide_left(project_all), wide_right(work[:, rank:]), (1, 0))
        lt[...] = turned
        load = turned.T
        ub[...] = ub[...] + delta
        if sweep == SWEEPS - 1:
            fac_out[...] = factors + after["shift"]
        links.settle()

    load_out[...] = load
    unit_out[...] = ub[...].T[0:1, :]
    for c in range(nx):
        day_out[:, c * chunk:(c + 1) * chunk] = bd[c]


def deliver(*refs):
    for source, target in zip(refs[:4], refs[4:]):
        target[...] = source[...]


def body(shape, panel, treat_start, loading_init, factor_init, unit_init, day_init):
    units, days = panel.shape
    rank, w = factor_init.shape
    nx, ny, nz = (shape[axis] for axis in AXES)
    chunk = days // nx
    high = rank + 1
    each = rank * rank // LANES + 8
    places = nx + ny + nz
    count = SWEEPS * (2 * places + nx * (ny + nz + 1)) + (SWEEPS + 1) * nx * (ny + nz + 1)
    dma = pltpu.SemaphoreType.DMA

    def array(*sizes):
        return jax.ShapeDtypeStruct(sizes, F32)

    outs = (array(rank, units), array(rank, w), array(1, units), array(1, days))
    results = pl.pallas_call(
        functools.partial(kernel, shape),
        out_shape=outs,
        in_specs=[ANY] + [VMEM] * 5,
        out_specs=(VMEM,) * 4,
        scratch_shapes=[
            pltpu.VMEM((nx, units, chunk), F32),
            pltpu.VMEM((nx, units, chunk), BF16),
            pltpu.VMEM((nx, units, chunk), BF16),
            pltpu.VMEM((SWEEPS + 1, nx, ny, nz, high, w), F32),
            pltpu.VMEM((nx, rank, chunk), BF16),
            pltpu.VMEM((nx, rank, chunk), BF16),
            pltpu.VMEM((nx, 1, chunk), F32),
            pltpu.VMEM((nx, nz, ny, high, w), F32),
            pltpu.VMEM((SWEEPS, nz, nx, ny, high, w), F32),
            pltpu.VMEM((SWEEPS, ny, nx, high, w), F32),
            pltpu.VMEM((SWEEPS, nx, high, w), F32),
            pltpu.VMEM((nx, ny, high, w), F32),
            pltpu.VMEM((nx, high, w), F32),
            pltpu.VMEM((SWEEPS, places, each, LANES), F32),
            pltpu.VMEM((SWEEPS, places, 8, LANES), F32),
            pltpu.VMEM((units, rank), F32),
            pltpu.VMEM((units, 3 * rank), BF16),
            pltpu.VMEM((2 * rank, units), BF16),
            pltpu.VMEM((units, LANES), F32),
            pltpu.VMEM((units, LANES), F32),
            pltpu.VMEM((units, LANES), F32),
            dma((nx,)),
            dma((count,)),
            dma((count,)),
        ],
        compiler_params=pltpu.CompilerParams(collective_id=0, has_side_effects=True, vmem_limit_bytes=60 * 1024 * 1024),
        name="sweeps",
    )(panel, treat_start[None, :], loading_init, factor_init, unit_init[None, :], day_init[None, :])
    loading, factors, unit_eff, day_eff = pl.pallas_call(
        deliver, out_shape=outs, in_specs=[VMEM] * 4, out_specs=(VMEM,) * 4, name="deliver")(*results)
    return (loading, factors, unit_eff[0], day_eff[0])


def solution(mesh):
    return jax.shard_map(
        functools.partial(body, dict(mesh.shape)),
        mesh=mesh,
        in_specs=(P(AXES, None), P(AXES), P(None, AXES), P(None, AXES), P(AXES), P()),
        out_specs=(P(None, AXES), P(None, AXES), P(AXES), P()),
        check_vma=False,
    )
```

time: 105 us -> 77.3 us (0.74)
  Pallas kernels: 98 us -> 76.5 us
  local copies, waits for them, and re-layouts: 5.39 us -> 0 us
    pallas_call x1 -> x2, Pallas kernels: 98 us -> 76.5 us  [the longest x1 75 us: body(): pl.pallas_call(functools.partial(kernel, shape), out_shape=outs, in_specs...]
    unnamed x4 -> x0, local copies, waits for them, and re-layouts: 5.39 us -> none
where the time goes in v2:
time: 77.3 us; the launch traced here: 77.1 us
  Pallas kernels  76.5 us (99%)
    pallas_call x1, Pallas kernels, body(): pl.pallas_call(functools.partial(kernel, shape), out_shape=outs, in_specs...  75 us

profile of v2, /device:TPU:1, one launch (start us, length us, event | category | flops | bytes accessed | tf_op | source)
XLA Modules:
  0.0 77.1 jit_solution(2249814733054985525)
XLA Ops:
  0.6 75.0 %sweeps.1 = (f32[64,256]{1,0:T(8,128)}, f32[64,128]{1,0:T(8,128)}, f32[1,256]{1,0:T(1,128)}, f32[1,4096]{1,0:T(1,128)}) custom-call(f32[256,4096]{1,0:T(8,128)} %panel_ref.1, s32[1,256]{1,0:T(1,128)} %bitcast.6, f32[64,256]{1,0:T(8,128)} %load_ref.1, f32[64,128]{1,0:T(8,128)} %fac_ref.1, f32[1,256]{1,0:T(1,128)} %bitcast.7, f32[1,4096]{1,0:T(1,128)} %bitcast.5), custom_call_target="tpu_custom_call" | custom-call | tf_op jit(solution)/shard_map/sweeps/pallas_call | solution.py:487
  75.6 1.5 %deliver.1 = (f32[64,256]{1,0:T(8,128)}, f32[64,128]{1,0:T(8,128)}, f32[1,256]{1,0:T(1,128)}, f32[1,4096]{1,0:T(1,128)}) custom-call(f32[64,256]{1,0:T(8,128)} %get-tuple-element.12.refs_0_, f32[64,128]{1,0:T(8,128)} %get-tuple-element.13.refs_1_, f32[1,256]{1,0:T(1,128)} %get-tuple-element.14.refs_2_, f32[1,4096]{1,0:T(1,128)} %get-tuple-element.15.refs_3_), custom_call_target="tpu_custom_call" | custom-call | tf_op jit(solution)/shard_map/deliver/pallas_call | solution.py:521

commit v3 on v2

--- a/solution.py
+++ b/solution.py
@@ -75,24 +75,49 @@
 
 
 def eliminate(work, first, last):
-    row_at = lax.broadcasted_iota(jnp.int32, work.shape, 0)
+    rank, span = work.shape
+    shape = (8, span)
+    row_at = lax.broadcasted_iota(jnp.int32, shape, 0)
+    tiles = [work[8 * u:8 * u + 8] for u in range(rank // 8)]
+    four = range(4)
+
+    def row(value, at):
+        return jnp.broadcast_to(value[at:at + 1], shape)
+
+    def lane(value, at):
+        return jnp.broadcast_to(value[:, at:at + 1], shape)
+
+    def combine(factors, values):
+        return (factors[0] * values[0] + factors[1] * values[1]) + (factors[2] * values[2] + factors[3] * values[3])
+
+    block = None
     for k in range(4 * first, 4 * last, 4):
-        cols = [jnp.broadcast_to(work[:, k + i:k + i + 1], work.shape) for i in range(4)]
-        rows = [work[k + i:k + i + 1] for i in range(4)]
-        block = quad_inverse([[cols[j][k + i:k + i + 1] for j in range(4)] for i in range(4)])
-        pivots = [(b[0] * rows[0] + b[1] * rows[1]) + (b[2] * rows[2] + b[3] * rows[3]) for b in block]
-        work = work - (cols[0] * pivots[0] + cols[1] * pivots[1]) - (cols[2] * pivots[2] + cols[3] * pivots[3])
-        for i in range(4):
-            work = jnp.where(row_at == k + i, pivots[i], work)
-    return work
+        here, at = k // 8, k % 8
+        cols = [[lane(tile, k + i) for tile in tiles] for i in four]
+        rows = [row(tiles[here], at + i) for i in four]
+        if block is None:
+            block = [[row(cols[j][here], at + i) for j in four] for i in four]
+        inverse = quad_inverse(block)
+        if k + 4 < 4 * last:
+            there, to = (k + 4) // 8, (k + 4) % 8
+            ahead = [[lane(rows[i], k + 4 + c) for i in four] for c in four]
+            old = [[lane(row(tiles[there], to + i), k + 4 + c) for c in four] for i in four]
+            side = [[row(cols[j][there], to + i) for j in four] for i in four]
+            near = [[combine(inverse[j], ahead[c]) for j in four] for c in four]
+            block = [[old[i][c] - combine(side[i], near[c]) for c in four] for i in four]
+        pivots = [combine(inverse[i], rows) for i in four]
+        tiles = [tile - combine([cols[i][u] for i in four], pivots) for u, tile in enumerate(tiles)]
+        for i in four:
+            tiles[here] = jnp.where(row_at == at + i, pivots[i], tiles[here])
+    return jnp.concatenate(tiles, 0)
 
 
 def column(row, rank):
     return jnp.sum(jnp.where(eye(rank), row, 0.0), 1, keepdims=True)
 
 
-def nearest(here, count):
-    lists = [sorted(range(count), key=lambda at: (abs(at - place), at)) for place in range(count)]
+def ranked(here, count, cost):
+    lists = [sorted(range(count), key=lambda at: (cost(place, at), at)) for place in range(count)]
     found = []
     for rank in range(count):
         value = lists[0][rank]
@@ -100,6 +125,14 @@
             value = jnp.where(here == place, lists[place][rank], value)
         found.append(value)
     return found
+
+
+def apart(left, right):
+    return abs(left - right)
+
+
+def bits_alike(left, right):
+    return -bin(left ^ right).count("1")
 
 
 class Exchange:
@@ -128,6 +161,7 @@
         self.here = {axis: lax.axis_index(axis) for axis in AXES}
         self.others = {
             axis: [lax.rem(self.here[axis] + step, shape[axis]) for step in range(1, shape[axis])] for axis in AXES}
+        self.others["gy"] = ranked(self.here["gy"], shape["gy"], bits_alike)[:-1]
         self.index, self.open = 0, []
 
     def take(self, count):
@@ -137,14 +171,14 @@
     def device(self, axis, there):
         return tuple(there if name == axis else self.here[name] for name in AXES)
 
-    def meet(self):
+    def greet(self):
         barrier = pltpu.get_barrier_semaphore()
-        count = 0
         for axis in AXES:
             for there in self.others[axis]:
                 pl.semaphore_signal(barrier, inc=1, device_id=self.device(axis, there), device_id_type=MESH)
-                count += 1
-        pl.semaphore_wait(barrier, count)
+
+    def meet(self):
+        pl.semaphore_wait(pltpu.get_barrier_semaphore(), sum(len(self.others[axis]) for axis in AXES))
 
     def settle(self):
         for copy in self.open:
@@ -185,7 +219,7 @@
 def kernel(shape, panel_ref, treat_ref, load_ref, fac_ref, unit_ref, day_ref,
            load_out, fac_out, unit_out, day_out,
            pan, xh, xl, blocks, fh, fl, bd, part, hold_z, hold_y, hold_x, sum_z, sum_y,
-           gram_hold, tail_hold, lt, lw, ls, limit, ub, rsum, local, send, recv):
+           gram_hold, tail_hold, ld, tr, ur, dr, wide, lt, lw, ls, limit, ub, rsum, local, small, send, recv):
     nx, ny, nz = (shape[axis] for axis in AXES)
     devices = nx * ny * nz
     units, days = panel_ref.shape
@@ -202,14 +236,17 @@
         return pltpu.make_async_copy(
             panel_ref.at[:, pl.ds(pl.multiple_of(at * chunk, chunk), chunk)], pan.at[at], local.at[at])
 
+    links.greet()
+    inputs = [
+        pltpu.make_async_copy(source, target, small.at[n]) for n, (source, target) in enumerate((
+            (load_ref, ld), (fac_ref, blocks.at[0, x, y, z, 0:rank]), (treat_ref, tr), (unit_ref, ur), (day_ref, dr)))]
+    for copy in inputs:
+        copy.start()
     for c in range(nx):
         fetch(c).start()
-    blocks[0, x, y, z, 0:rank, :] = fac_ref[...]
-    links.meet()
-
-    line = nearest(x, nx)
-
-    def gather(buf, rows, consume):
+    line = ranked(x, nx, apart)
+
+    def gather(buf, rows, consume, meanwhile):
         def spot(at, j):
             return buf.at[at, j, z, 0:rows] if rows < buf.shape[3] else buf.at[at, j, z]
 
@@ -226,11 +263,13 @@
             place = pair_spot(line[n])
             zs.append(Exchange(links, "gz", links.others["gz"], lambda there: place(z), place))
 
+        xs = Exchange(links, "gx", line[1:], lambda there: spot(x, y), lambda i: spot(i, y))
         spread(x)
-        xs = Exchange(links, "gx", line[1:], lambda there: spot(x, y), lambda i: spot(i, y))
-        for at in line[1:]:
+        for n, at in enumerate(line[1:]):
+            meanwhile(n)
             xs.wait(at)
             spread(at)
+        meanwhile(nx - 1)
         pair(0)
         for n in range(nx):
             if n + 1 < nx:
@@ -238,29 +277,45 @@
             zs[n].wait(*links.others["gz"])
             consume(n, line[n])
 
-    def take(buf, at, shift):
-        found = []
-        for j in range(ny):
-            for k in range(nz):
-                c = (j * nz + k) * w
-                block = buf[at, j, k, 0:rank, :]
-                if shift is not None:
-                    block = block + shift
-                high, low = halves(block)
-                fh[at, :, c:c + w] = high
-                fl[at, :, c:c + w] = low
-                found.append(block)
-        return found
-
-    load = load_ref[...]
-    flip = jnp.broadcast_to(unit_ref[...], (LANES, units)).T
-    ub[...] = flip
+    def collect(buf, at, rows):
+        parts = [buf[at, j, k, 0:rows, :] for j in range(ny) for k in range(nz)]
+        if w % LANES == 0:
+            return jnp.concatenate(parts, 1)
+        for c, part_value in enumerate(parts):
+            wide[0:rows, c * w:(c + 1) * w] = part_value
+        return wide[0:rows, :]
+
+    def take(at, value):
+        high, low = halves(value)
+        fh[at] = high
+        fl[at] = low
+
+    each = rank // fold
+
+    def prepare(load, turned):
+        lt[...] = turned
+        lw[...] = wide_left(turned)
+        high, low = halves(load)
+        stack = jnp.concatenate([high, low], 0)
+        ls[...] = stack
+        gram = quadrants(mul(stack, stack, (1, 1)), rank, rank)
+        packed = jnp.concatenate([gram[f * each:(f + 1) * each] for f in range(fold)], 1)
+        return packed, jnp.sum(turned, 0, keepdims=True)
+
+    def lanes(row):
+        return jnp.concatenate([row, jnp.zeros((1, LANES - rank), F32)], 1) if rank < LANES else row
+
+    inputs[0].wait()
+    message = prepare(ld[...], ld[...].T)
+    inputs[2].wait()
+    inputs[3].wait()
+    inputs[4].wait()
+    ub[...] = jnp.broadcast_to(ur[...], (LANES, units)).T
     lane = lax.broadcasted_iota(jnp.int32, (units, LANES), 1).astype(F32)
-    limit[...] = jnp.broadcast_to(treat_ref[...].astype(F32), (LANES, units)).T - lane
+    limit[...] = jnp.broadcast_to(tr[...].astype(F32), (LANES, units)).T - lane
     for c in range(nx):
-        bd[c] = day_ref[:, c * chunk:(c + 1) * chunk]
+        bd[c] = dr[:, c * chunk:(c + 1) * chunk]
     row_at = lax.broadcasted_iota(jnp.int32, (8, LANES), 0)
-    pad = jnp.zeros((8, LANES - rank), F32)
 
     def impute(at):
         def tile(t, _):
@@ -300,21 +355,15 @@
         lax.fori_loop(0, chunk // width, tile, 0)
 
     for sweep in range(SWEEPS):
-        if sweep == 0:
-            lt[...] = load.T
-        turned = lt[...]
-        lw[...] = wide_left(turned)
-        high, low = halves(load)
-        stack = jnp.concatenate([high, low], 0)
-        ls[...] = stack
-        gram = quadrants(mul(stack, stack, (1, 1)), rank, rank)
-        each = rank // fold
-        packed = jnp.concatenate([gram[f * each:(f + 1) * each] for f in range(fold)], 1)
-        load_sum = jnp.sum(turned, 0, keepdims=True)
-        load_sum = jnp.concatenate([load_sum, jnp.zeros((1, LANES - rank), F32)], 1) if rank < LANES else load_sum
+        packed, load_sum = message
         unit_sum = jnp.sum(ub[:, 0:1], 0, keepdims=True)
-        extra = jnp.where(row_at == 0, load_sum, jnp.where(row_at == 1, unit_sum, 0.0))
-        grams = SmallSum(links, gram_hold.at[sweep], jnp.concatenate([packed, extra], 0))
+        extra = jnp.where(row_at == 0, lanes(load_sum), jnp.where(row_at == 1, unit_sum, 0.0))
+        grams = []
+
+        def add_grams(n=0):
+            if n == 0:
+                grams.append(SmallSum(links, gram_hold.at[sweep], jnp.concatenate([packed, extra], 0)))
+
         rsum[...] = jnp.zeros_like(rsum)
         hz, hy, hx = hold_z.at[sweep], hold_y.at[sweep], hold_x.at[sweep]
         order = line if sweep == 0 else line[:0:-1] + line[:1]
@@ -362,47 +411,34 @@
             if n >= 1:
                 across(n - 1)
             if n == 0:
-                grams.step()
+                grams[0].step()
 
         if sweep == 0:
             def begin(n, at):
-                take(blocks.at[0], at, None)
+                take(at, collect(blocks.at[0], at, rank))
                 chunk_step(n)
 
-            gather(blocks.at[0], rank, begin)
+            links.meet()
+            inputs[1].wait()
+            gather(blocks.at[0], rank, begin, add_grams)
         else:
+            add_grams()
             for n in range(nx):
                 chunk_step(n)
 
         rows = jnp.sum(rsum[...], 1, keepdims=True)
-        weighted_rows = jnp.sum(turned * rows, 0, keepdims=True)
-        if rank < LANES:
-            weighted_rows = jnp.concatenate([weighted_rows, jnp.zeros((1, LANES - rank), F32)], 1)
+        weighted_rows = lanes(jnp.sum(lt[...] * rows, 0, keepdims=True))
         row_total = jnp.sum(rows, 0, keepdims=True)
         tails = SmallSum(
             links, tail_hold.at[sweep], jnp.where(row_at == 0, weighted_rows, jnp.where(row_at == 1, row_total, 0.0)))
-        grams.step()
+        grams[0].step()
         across(nx - 1)
         tails.step()
-
-        def pass_on(n):
+        for n in range(nx):
             along(n)
             if n != local_piece:
                 forward(n)
-
-        for n in range(nx - 2):
-            pass_on(n)
-        gram_all = grams.finish()
-        work = jnp.concatenate([gram_all[0:each, f * rank:(f + 1) * rank] for f in range(fold)], 0)
-        work = eliminate(with_identity(work), 0, rank // 8)
-        pass_on(nx - 2)
         tails.step()
-        work = eliminate(work, rank // 8, rank // 4)
-        pass_on(nx - 1)
-        inverse = wide_left(work[:, rank:])
-        sum_l = column(gram_all[each:each + 1, 0:rank], rank)
-        old_units = gram_all[each + 1:each + 2, 0:1] / total_units
-        old_days = sum(jnp.sum(bd[c], 1, keepdims=True) for c in range(nx)) / days
         for at in line[1:]:
             pltpu.make_async_remote_copy(
                 hx.at[at], hx.at[at], send.at[last_base], recv.at[last_base + at],
@@ -410,39 +446,54 @@
         value = sum_y[x]
         for at in line[1:]:
             value = value + hx[at]
-        moved = value[rank:rank + 1, :] / total_units
-        factors = mul(inverse, wide_right(value[0:rank, :] + sum_l * (old_units + old_days - moved)), (1, 0))
-        own = blocks.at[sweep + 1, x, y, z]
-        own[0:rank, :] = factors
-        own[rank:rank + 1, :] = moved - old_days
         buf = blocks.at[sweep + 1]
-        sums, after = {}, {}
+        buf[x, y, z] = value
+        held, sums = {}, {}
+
+        def solve_grams(n):
+            if n == 0:
+                gram_all = grams[0].finish()
+                work = jnp.concatenate([gram_all[0:each, f * rank:(f + 1) * rank] for f in range(fold)], 0)
+                held["work"] = with_identity(work)
+                held["load"] = column(gram_all[each:each + 1, 0:rank], rank)
+                held["units"] = gram_all[each + 1:each + 2, 0:1] / total_units
+                held["days"] = sum(jnp.sum(bd[c], 1, keepdims=True) for c in range(nx)) / days
+            quads = rank // 4
+            cuts = [0, quads // 2] + [quads - quads // 2 + quads // 2 * i // (nx - 1) for i in range(1, nx)]
+            held["work"] = eliminate(held["work"], cuts[n], cuts[n + 1])
+            if n == nx - 1:
+                held["inverse"] = wide_left(held["work"][:, rank:])
 
         def keep(name, value):
             sums[name] = sums[name] + value if name in sums else value
+
+        def solve(sums_at):
+            day_sums = sums_at[rank:rank + 1, :] / total_units
+            right = sums_at[0:rank, :] + held["load"] * (held["level"] - day_sums) - held["rows"]
+            return mul(held["inverse"], wide_right(right), (1, 0)), day_sums - (held["days"] + held["mean"])
 
         def project(n, at):
             if n == 0:
                 tail_all = tails.finish()
-                mean = tail_all[1:2, 0:1] / (total_units * days)
-                right = sum_l * (2.0 * mean) - column(tail_all[0:1, 0:rank], rank) / days
-                shift = mul(inverse, wide_right(jnp.broadcast_to(right, (rank, LANES))), (1, 0))[:, 0:1]
-                after.update(mean=mean, shift=shift, delta=rows / days - (mean + old_units))
-            found = take(buf, at, after["shift"])
+                held["mean"] = tail_all[1:2, 0:1] / (total_units * days)
+                held["rows"] = column(tail_all[0:1, 0:rank], rank) / days
+                held["level"] = held["units"] + held["days"] + 2.0 * held["mean"]
+                held["delta"] = rows / days - (held["mean"] + held["units"])
+                if sweep == SWEEPS - 1:
+                    fac_out[...] = solve(buf[x, y, z])[0]
+            factors, change = solve(collect(buf, at, rank + 1))
+            take(at, factors)
             both = jnp.concatenate([fh[at], fl[at]], 0)
             keep("square", mul(both, both, (1, 1)))
             keep("project", mul(xh[at], both, (1, 1)) + mul(xl[at], both, (1, 1)))
-            for j in range(ny):
-                for k in range(nz):
-                    c = (j * nz + k) * w
-                    change = buf[at, j, k, rank:rank + 1, :] - after["mean"]
-                    block = found[j * nz + k]
-                    keep("plain", block)
-                    keep("days", block * change)
-                    bd[at, :, c:c + w] = bd[at, :, c:c + w] + change
-
-        gather(buf, rank + 1, project)
-        delta = after["delta"]
+            moved = factors * change
+            for c in range(chunk // LANES):
+                keep("plain", factors[:, c * LANES:(c + 1) * LANES])
+                keep("days", moved[:, c * LANES:(c + 1) * LANES])
+            bd[at] = bd[at] + change
+
+        gather(buf, rank + 1, project, solve_grams)
+        delta = held["delta"]
         work = eliminate(with_identity(quadrants(sums["square"], rank, rank)), 0, rank // 4)
         day_term = jnp.sum(sums["days"], 1, keepdims=True)
         plain = jnp.sum(sums["plain"], 1, keepdims=True)
@@ -451,11 +502,10 @@
         project_all = sums["project"][:, :rank] + sums["project"][:, rank:]
         project_all = project_all - delta * plain_row - day_row
         turned = mul(wide_left(project_all), wide_right(work[:, rank:]), (1, 0))
-        lt[...] = turned
         load = turned.T
         ub[...] = ub[...] + delta
-        if sweep == SWEEPS - 1:
-            fac_out[...] = factors + after["shift"]
+        if sweep < SWEEPS - 1:
+            message = prepare(load, turned)
         links.settle()
 
     load_out[...] = load
@@ -487,7 +537,7 @@
     results = pl.pallas_call(
         functools.partial(kernel, shape),
         out_shape=outs,
-        in_specs=[ANY] + [VMEM] * 5,
+        in_specs=[ANY] * 6,
         out_specs=(VMEM,) * 4,
         scratch_shapes=[
             pltpu.VMEM((nx, units, chunk), F32),
@@ -505,6 +555,11 @@
             pltpu.VMEM((nx, high, w), F32),
             pltpu.VMEM((SWEEPS, places, each, LANES), F32),
             pltpu.VMEM((SWEEPS, places, 8, LANES), F32),
+            pltpu.VMEM((rank, units), F32),
+            pltpu.VMEM((1, units), jnp.int32),
+            pltpu.VMEM((1, units), F32),
+            pltpu.VMEM((1, days), F32),
+            pltpu.VMEM((high, chunk), F32),
             pltpu.VMEM((units, rank), F32),
             pltpu.VMEM((units, 3 * rank), BF16),
             pltpu.VMEM((2 * rank, units), BF16),
@@ -512,6 +567,7 @@
             pltpu.VMEM((units, LANES), F32),
             pltpu.VMEM((units, LANES), F32),
             dma((nx,)),
+            dma((5,)),
             dma((count,)),
             dma((count,)),
         ],

time: 77.3 us -> 72.4 us (0.937)
  Pallas kernels: 76.5 us -> 71.6 us
    pallas_call x1, Pallas kernels: 75 us -> 70.1 us  [body(): pl.pallas_call(functools.partial(kernel, shape), out_shape=outs, in_specs...]
where the time goes in v3:
time: 72.4 us; the launch traced here: 72.2 us
  Pallas kernels  71.6 us (99%)
    pallas_call x1, Pallas kernels, body(): pl.pallas_call(functools.partial(kernel, shape), out_shape=outs, in_specs...  70.1 us
    pallas_call x1, Pallas kernels, body(): pl.pallas_call(deliver, out_shape=outs, in_specs=[VMEM] * 4, out_specs=(V...  1.51 us

profile of v3, /device:TPU:1, one launch (start us, length us, event | category | flops | bytes accessed | tf_op | source)
XLA Modules:
  0.0 72.2 jit_solution(236923207108984026)
XLA Ops:
  0.6 70.1 %sweeps.1 = (f32[64,256]{1,0:T(8,128)}, f32[64,128]{1,0:T(8,128)}, f32[1,256]{1,0:T(1,128)}, f32[1,4096]{1,0:T(1,128)}) custom-call(f32[256,4096]{1,0:T(8,128)} %panel_ref.1, s32[1,256]{1,0:T(1,128)} %bitcast.6, f32[64,256]{1,0:T(8,128)} %load_ref.1, f32[64,128]{1,0:T(8,128)} %fac_ref.1, f32[1,256]{1,0:T(1,128)} %bitcast.7, f32[1,4096]{1,0:T(1,128)} %bitcast.5), custom_call_target="tpu_custom_call" | custom-call | tf_op jit(solution)/shard_map/sweeps/pallas_call | solution.py:537
  70.7 1.5 %deliver.1 = (f32[64,256]{1,0:T(8,128)}, f32[64,128]{1,0:T(8,128)}, f32[1,256]{1,0:T(1,128)}, f32[1,4096]{1,0:T(1,128)}) custom-call(f32[64,256]{1,0:T(8,128)} %get-tuple-element.12.refs_0_, f32[64,128]{1,0:T(8,128)} %get-tuple-element.13.refs_1_, f32[1,256]{1,0:T(1,128)} %get-tuple-element.14.refs_2_, f32[1,4096]{1,0:T(1,128)} %get-tuple-element.15.refs_3_), custom_call_target="tpu_custom_call" | custom-call | tf_op jit(solution)/shard_map/deliver/pallas_call | solution.py:577

commit v4 on v3

--- a/solution.py
+++ b/solution.py
@@ -9,7 +9,7 @@
 
 SWEEPS = 2
 RIDGE = 1.0
-WIDTH = 512
+WIDTH = 1024
 LANES = 128
 AXES = ("gx", "gy", "gz")
 MESH = pl.DeviceIdType.MESH
@@ -448,6 +448,7 @@
             value = value + hx[at]
         buf = blocks.at[sweep + 1]
         buf[x, y, z] = value
+        earlier, links.open = links.open, []
         held, sums = {}, {}
 
         def solve_grams(n):
@@ -463,6 +464,8 @@
             held["work"] = eliminate(held["work"], cuts[n], cuts[n + 1])
             if n == nx - 1:
                 held["inverse"] = wide_left(held["work"][:, rank:])
+                for copy in earlier:
+                    copy.wait_send()
 
         def keep(name, value):
             sums[name] = sums[name] + value if name in sums else value
@@ -506,12 +509,12 @@
         ub[...] = ub[...] + delta
         if sweep < SWEEPS - 1:
             message = prepare(load, turned)
-        links.settle()
 
     load_out[...] = load
     unit_out[...] = ub[...].T[0:1, :]
     for c in range(nx):
         day_out[:, c * chunk:(c + 1) * chunk] = bd[c]
+    links.settle()
 
 
 def deliver(*refs):

time: 72.4 us -> 71.2 us (0.983)
  Pallas kernels: 71.6 us -> 70.4 us
    pallas_call x1, Pallas kernels: 70.1 us -> 68.8 us  [body(): pl.pallas_call(functools.partial(kernel, shape), out_shape=outs, in_specs...]
where the time goes in v4:
time: 71.2 us; the launch traced here: 71 us
  Pallas kernels  70.4 us (99%)
    pallas_call x1, Pallas kernels, body(): pl.pallas_call(functools.partial(kernel, shape), out_shape=outs, in_specs...  68.8 us
    pallas_call x1, Pallas kernels, body(): pl.pallas_call(deliver, out_shape=outs, in_specs=[VMEM] * 4, out_specs=(V...  1.51 us

profile of v4, /device:TPU:1, one launch (start us, length us, event | category | flops | bytes accessed | tf_op | source)
XLA Modules:
  0.0 71.0 jit_solution(17177263298079769893)
XLA Ops:
  0.6 68.8 %sweeps.1 = (f32[64,256]{1,0:T(8,128)}, f32[64,128]{1,0:T(8,128)}, f32[1,256]{1,0:T(1,128)}, f32[1,4096]{1,0:T(1,128)}) custom-call(f32[256,4096]{1,0:T(8,128)} %panel_ref.1, s32[1,256]{1,0:T(1,128)} %bitcast.6, f32[64,256]{1,0:T(8,128)} %load_ref.1, f32[64,128]{1,0:T(8,128)} %fac_ref.1, f32[1,256]{1,0:T(1,128)} %bitcast.7, f32[1,4096]{1,0:T(1,128)} %bitcast.5), custom_call_target="tpu_custom_call" | custom-call | tf_op jit(solution)/shard_map/sweeps/pallas_call | solution.py:540
  69.5 1.5 %deliver.1 = (f32[64,256]{1,0:T(8,128)}, f32[64,128]{1,0:T(8,128)}, f32[1,256]{1,0:T(1,128)}, f32[1,4096]{1,0:T(1,128)}) custom-call(f32[64,256]{1,0:T(8,128)} %get-tuple-element.12.refs_0_, f32[64,128]{1,0:T(8,128)} %get-tuple-element.13.refs_1_, f32[1,256]{1,0:T(1,128)} %get-tuple-element.14.refs_2_, f32[1,4096]{1,0:T(1,128)} %get-tuple-element.15.refs_3_), custom_call_target="tpu_custom_call" | custom-call | tf_op jit(solution)/shard_map/deliver/pallas_call | solution.py:580

commit v5 on v4

--- a/solution.py
+++ b/solution.py
@@ -504,7 +504,10 @@
         plain_row = jnp.sum(jnp.where(eye(rank), plain, 0.0), 0, keepdims=True)
         project_all = sums["project"][:, :rank] + sums["project"][:, rank:]
         project_all = project_all - delta * plain_row - day_row
-        turned = mul(wide_left(project_all), wide_right(work[:, rank:]), (1, 0))
+        left_high, left_low = halves(project_all)
+        right_high, right_low = halves(work[:, rank:])
+        turned = mul(left_high, right_high, (1, 0)) + (
+            mul(left_high, right_low, (1, 0)) + mul(left_low, right_high, (1, 0)))
         load = turned.T
         ub[...] = ub[...] + delta
         if sweep < SWEEPS - 1:

time: 71.2 us -> 71.1 us (level)
  no operation moved by 1% of the time
where the time goes in v5:
time: 71.1 us; the launch traced here: 71 us
  Pallas kernels  70.3 us (99%)
    pallas_call x1, Pallas kernels, body(): pl.pallas_call(functools.partial(kernel, shape), out_shape=outs, in_specs...  68.8 us
    pallas_call x1, Pallas kernels, body(): pl.pallas_call(deliver, out_shape=outs, in_specs=[VMEM] * 4, out_specs=(V...  1.51 us

profile of v5, /device:TPU:1, one launch (start us, length us, event | category | flops | bytes accessed | tf_op | source)
XLA Modules:
  0.0 71.0 jit_solution(6366883850422574495)
XLA Ops:
  0.6 68.8 %sweeps.1 = (f32[64,256]{1,0:T(8,128)}, f32[64,128]{1,0:T(8,128)}, f32[1,256]{1,0:T(1,128)}, f32[1,4096]{1,0:T(1,128)}) custom-call(f32[256,4096]{1,0:T(8,128)} %panel_ref.1, s32[1,256]{1,0:T(1,128)} %bitcast.6, f32[64,256]{1,0:T(8,128)} %load_ref.1, f32[64,128]{1,0:T(8,128)} %fac_ref.1, f32[1,256]{1,0:T(1,128)} %bitcast.7, f32[1,4096]{1,0:T(1,128)} %bitcast.5), custom_call_target="tpu_custom_call" | custom-call | tf_op jit(solution)/shard_map/sweeps/pallas_call | solution.py:543
  69.5 1.5 %deliver.1 = (f32[64,256]{1,0:T(8,128)}, f32[64,128]{1,0:T(8,128)}, f32[1,256]{1,0:T(1,128)}, f32[1,4096]{1,0:T(1,128)}) custom-call(f32[64,256]{1,0:T(8,128)} %get-tuple-element.12.refs_0_, f32[64,128]{1,0:T(8,128)} %get-tuple-element.13.refs_1_, f32[1,256]{1,0:T(1,128)} %get-tuple-element.14.refs_2_, f32[1,4096]{1,0:T(1,128)} %get-tuple-element.15.refs_3_), custom_call_target="tpu_custom_call" | custom-call | tf_op jit(solution)/shard_map/deliver/pallas_call | solution.py:583
